TPU v7x, 512 devices: a whole 4x4x16 slice. The times are simulated.
512 devices in a mesh: seq: 128 (over x, z, core), head: 4 (over y).
Axes of the slice: x: 4, y: 4, z: 16, core: 2. Of those that a mesh axis runs over, the one named last changes fastest.
Arguments:
- q_raw: bfloat16 [65536, 4096], P('seq', 'head'), may hold values from -120 to 120
- k_raw: bfloat16 [65536, 4096], P('seq', 'head'), may hold values from -6 to 6
- v_raw: bfloat16 [65536, 4096], P('seq', 'head'), may hold values from -6 to 6
- block_scales: float32 [3, 512, 32], P(None, 'seq', 'head'), may hold values from 0.25 to 4
- segment_ids: int32 [65536], P('seq'), may hold values from 0 to 504, as said below
- norm_gain: float32 [4096], P('head'), may hold values from 0.5 to 1.5
Outputs:
- attended: bfloat16 [65536, 4096], P('seq', 'head')
Inputs may be any that keep to these rules, and one draw needn't show every extreme that they name: `segment_ids`: ids start at 0 and never fall, rising by at most one from a token to the next. Each aligned block of 512 tokens has exactly 4 segment starts, except the second and third blocks, which have none; in the second-to-last block all starts lie in the block's first half, in the last block all lie in its second half. No segment starts at the first token of a block except segment 0 at token 0.
All inputs are finite; a program needn't handle non-finite values.
Results may differ from a plain program's by a relative error of at most 0.013.
Values may be sent and summed in bfloat16 or wider, within the bound.
A program may use at most 64 MiB of HBM per device.

v0:
```python
import jax
import jax.numpy as jnp
from jax import lax
from jax.sharding import Mesh
from jax.sharding import PartitionSpec as P

H = 32
HD = 128
CAP = 4
SEQ = ("seq_0", "seq_1", "seq_2")


epsilon = 1e-06
missing_id = 1073741824.0


def neutral_like(array, identity):
    return jax.tree.map(
        lambda part, zero: jnp.zeros_like(part) + jnp.asarray(zero, part.dtype), array, identity
    )


def all_in_one(array, axis):
    leaves = jax.tree.leaves(array)
    sequence = sorted(range(len(leaves)), key=lambda k: -leaves[k].size)
    width = (1, *leaves[sequence[0]].shape)[-1]
    lines = [
        jnp.pad(leaves[k].reshape(-1), (0, -leaves[k].size % width)).reshape(-1, width)
        for k in sequence
    ]
    both, at, found = (lax.all_gather(jnp.concatenate(lines), axis), 0, {})
    for k, line in zip(sequence, lines):
        piece = both[:, at : at + len(line)].reshape(len(both), -1)
        found[k] = piece[:, : leaves[k].size].reshape(-1, *leaves[k].shape)
        at += len(line)
    numbers = iter(range(len(leaves)))
    return jax.tree.map(lambda _: found[next(numbers)], array)


def carried_in(array, axes, combine, identity):
    before = start = neutral_like(array, identity)
    subtotal = array
    for axis in reversed(axes):
        peers, place = (lax.axis_size(axis), lax.axis_index(axis))
        pieces = all_in_one(subtotal, axis)
        inside, subtotal = (start, start)
        for k in range(peers):
            passed = k < place
            subtotal = combine(subtotal, jax.tree.map(lambda part: part[k], pieces))
            inside = jax.tree.map(lambda new, old: jnp.where(passed, new, old), subtotal, inside)
        before = combine(inside, before)
    return before


def side_by_side(arrays, axis, dim, along):
    ends, at = ([], 0)
    for a in arrays[:-1]:
        at += a.shape[along]
        ends.append(at)
    both = jnp.concatenate(arrays, axis=along)
    return tuple(jnp.split(lax.all_gather(both, axis, axis=dim, tiled=True), ends, axis=along))


def rows_first(arrays, axis, dims):
    turned = [jnp.moveaxis(a, dim, 0) for a, dim in zip(arrays, dims)]
    widths = [t[0].size for t in turned]
    both = jnp.concatenate([t.reshape(-1, w) for t, w in zip(turned, widths)], axis=1)
    out = lax.all_gather(both, axis, axis=0, tiled=True)
    pieces = jnp.split(out, [sum(widths[:k]) for k in range(1, len(widths))], axis=1)
    return tuple(
        (
            jnp.moveaxis(b.reshape(-1, *t.shape[1:]), 0, dim)
            for b, t, dim in zip(pieces, turned, dims)
        )
    )


def shifted(block, axis, distance):
    devices = range(lax.axis_size(axis))
    route = [(i - distance, i) for i in devices if i - distance in devices]
    return lax.ppermute(block, axis, route)


def sent_to_all(array, axis):
    peers = lax.axis_size(axis)
    return lax.all_to_all(
        jnp.broadcast_to(array[None], (peers, *array.shape)), axis, 0, 0, tiled=True
    )


def taken_together(array, axis):
    return sent_to_all(array, axis).sum(axis=0)


def tail_combine(earlier, later):
    early_all, early_sum, early_count = earlier
    late_all, late_sum, late_count = later
    return (
        early_all * late_all,
        late_sum + late_all * early_sum,
        late_count + late_all * early_count,
    )


def finish_landmarks(part_key, part_value, part_count, carry_sum, carry_count):
    slot_index = jnp.arange(CAP, dtype=jnp.int32)
    lead_row = (slot_index == 0).astype(jnp.float32)
    key_total = part_key + lead_row[:, None] * carry_sum[..., 0:1, :]
    value_total = part_value + lead_row[:, None] * carry_sum[..., 1:2, :]
    count_total = part_count + lead_row * carry_count[..., 0]
    slot_size = jnp.maximum(count_total, 1.0)
    land_key = (key_total / slot_size[..., None]).astype(jnp.bfloat16)
    land_value = (value_total / slot_size[..., None]).astype(jnp.bfloat16)
    return (land_key, land_value, jnp.log(slot_size))


def on_device(q_raw, k_raw, v_raw, block_scales, segment_ids, norm_gain):
    token_count, width_total = q_raw.shape
    head_count = block_scales.shape[2]
    head_dim = width_total // head_count
    scale_block = token_count // block_scales.shape[1]
    half_len = token_count // 2
    score_scale = 1.0 / HD**0.5

    def dequantize(raw, which):
        factor = jnp.repeat(jnp.repeat(block_scales[which], scale_block, axis=0), head_dim, axis=1)
        return (raw.astype(jnp.float32) * factor).astype(jnp.bfloat16)

    queries = dequantize(q_raw, 0)
    keys_local = dequantize(k_raw, 1)
    values_local = dequantize(v_raw, 2)
    first_id = segment_ids[0]
    local_seg = segment_ids - first_id
    end_count = segment_ids[token_count - 1] - first_id
    slot_index = jnp.arange(CAP, dtype=jnp.int32)
    slot_pick = (local_seg[None, :] == slot_index[:, None]).astype(jnp.bfloat16)
    part_key = jnp.dot(slot_pick, keys_local, preferred_element_type=jnp.float32)
    part_value = jnp.dot(slot_pick, values_local, preferred_element_type=jnp.float32)
    part_count = jnp.sum(slot_pick.astype(jnp.float32), axis=1)
    in_tail = local_seg == end_count
    tail_row = in_tail.astype(jnp.bfloat16)[None, :]
    tail_sum = jnp.concatenate(
        [
            jnp.dot(tail_row, keys_local, preferred_element_type=jnp.float32),
            jnp.dot(tail_row, values_local, preferred_element_type=jnp.float32),
        ],
        axis=0,
    )
    tail_count = jnp.sum(in_tail.astype(jnp.float32)).reshape(1, 1)
    all_one = (end_count == 0).astype(jnp.float32).reshape(1, 1)
    slot_ids = jnp.where(
        slot_index < end_count, (first_id + slot_index).astype(jnp.float32), missing_id
    )
    starting = (
        jnp.ones((1, 1), jnp.float32),
        jnp.zeros((2, width_total), jnp.float32),
        jnp.zeros((1, 1), jnp.float32),
    )
    carried = carried_in((all_one, tail_sum, tail_count), SEQ, tail_combine, starting)
    carry_sum, carry_count = (carried[1], carried[2])
    own_key, own_value, own_bias = finish_landmarks(
        part_key, part_value, part_count, carry_sum, carry_count
    )
    table_key, table_value = side_by_side((own_key, own_value), SEQ, 0, 1)
    table_bias, table_ids = rows_first((own_bias, slot_ids), SEQ, (0, 0))
    rim_key = keys_local[token_count - half_len :]
    rim_value = values_local[token_count - half_len :]
    rim_mask = in_tail[token_count - half_len :].astype(jnp.bfloat16)
    prev_key, prev_value, prev_mask = shifted((rim_key, rim_value, rim_mask), SEQ, 1)
    prev_row = prev_mask[None, :]
    prev_sum = jnp.concatenate(
        [
            jnp.dot(prev_row, prev_key, preferred_element_type=jnp.float32),
            jnp.dot(prev_row, prev_value, preferred_element_type=jnp.float32),
        ],
        axis=0,
    )
    prev_count = jnp.sum(prev_mask.astype(jnp.float32))
    early_count = carry_count[0, 0] - prev_count
    later_count = carry_count[0, 0]
    early_mean = (carry_sum - prev_sum) / jnp.maximum(early_count, 1.0)
    later_mean = carry_sum / jnp.maximum(later_count, 1.0)
    positions = jnp.arange(token_count, dtype=jnp.int32)
    first_block = positions < half_len
    run_total = jnp.where(local_seg == 0, jnp.where(first_block, early_count, later_count), 0.0)
    run_live = run_total > 0.5
    run_log = jnp.log(jnp.maximum(run_total, 1.0))
    ext_ids = jnp.concatenate([jnp.where(prev_mask > 0, 0, -1).astype(jnp.int32), local_seg])
    ext_pos = jnp.arange(half_len + token_count, dtype=jnp.int32)
    win_mask = (
        (ext_ids[None, :] == local_seg[:, None])
        & (ext_pos[None, :] - half_len <= positions[:, None])
        & (ext_pos[None, :] // half_len >= positions[:, None] // half_len)
    )
    land_mask = table_ids[None, :] < segment_ids.astype(jnp.float32)[:, None]

    def by_head(matrix):
        return jnp.transpose(matrix.reshape(matrix.shape[0], head_count, head_dim), (1, 0, 2))

    head_items = (
        by_head(queries),
        by_head(jnp.concatenate([prev_key, keys_local], axis=0)),
        by_head(jnp.concatenate([prev_value, values_local], axis=0)),
        by_head(table_key),
        by_head(table_value),
        by_head(early_mean),
        by_head(later_mean),
    )

    def per_head(items):
        head_query, head_key, head_value, land_key, land_value, early_head, later_head = items
        win_score = (
            jnp.einsum("td,sd->ts", head_query, head_key, preferred_element_type=jnp.float32)
            * score_scale
        )
        win_score = jnp.where(win_mask, win_score, -jnp.inf)
        land_score = (
            jnp.einsum("td,sd->ts", head_query, land_key, preferred_element_type=jnp.float32)
            * score_scale
            + table_bias[None, :]
        )
        land_score = jnp.where(land_mask, land_score, -jnp.inf)
        rows_key = jnp.where(first_block[:, None], early_head[0][None, :], later_head[0][None, :])
        rows_value = jnp.where(first_block[:, None], early_head[1][None, :], later_head[1][None, :])
        run_score = (
            jnp.sum(head_query.astype(jnp.float32) * rows_key, axis=1) * score_scale + run_log
        )
        run_score = jnp.where(run_live, run_score, -jnp.inf)
        row_max = jnp.maximum(
            jnp.maximum(jnp.max(win_score, axis=1), jnp.max(land_score, axis=1)), run_score
        )
        win_weight = jnp.exp(win_score - row_max[:, None])
        land_weight = jnp.exp(land_score - row_max[:, None])
        run_weight = jnp.exp(run_score - row_max)
        row_total = jnp.sum(win_weight, axis=1) + jnp.sum(land_weight, axis=1) + run_weight
        weighted = jnp.einsum(
            "ts,sd->td",
            win_weight.astype(jnp.bfloat16),
            head_value,
            preferred_element_type=jnp.float32,
        )
        weighted = weighted + jnp.einsum(
            "ts,sd->td",
            land_weight.astype(jnp.bfloat16),
            land_value,
            preferred_element_type=jnp.float32,
        )
        weighted = weighted + run_weight[:, None] * rows_value
        return weighted / row_total[:, None]

    attention = lax.map(per_head, head_items)
    square_sum = jnp.sum(attention * attention, axis=(0, 2))
    square_total = taken_together(square_sum, "head")
    norm_scale = lax.rsqrt(square_total / (H * HD) + epsilon)
    flat = jnp.transpose(attention, (1, 0, 2)).reshape(token_count, width_total)
    return (flat * norm_scale[:, None] * norm_gain[None, :]).astype(jnp.bfloat16)


def solution(mesh):
    split = Mesh(
        mesh.devices.reshape(4, 16, 2, mesh.shape["head"]), ("seq_0", "seq_1", "seq_2", "head")
    )
    in_specs = (
        P(SEQ, "head"),
        P(SEQ, "head"),
        P(SEQ, "head"),
        P(None, SEQ, "head"),
        P(SEQ),
        P("head"),
    )
    out_specs = P(SEQ, "head")
    return jax.shard_map(
        on_device, mesh=split, in_specs=in_specs, out_specs=out_specs, check_vma=False
    )
```

profile of v0, /device:TPU:1, one launch (start us, length us, event | category | flops | bytes accessed | tf_op | source)
XLA Modules:
  0.0 356.8 jit_solution(9907449941974330395)
XLA Ops:
  9.2 1.9 convert_reduce_fusion.1
  15.7 8.3 %all-gather.3 = f32[2,4,1024]{2,1,0:T(4,128)S(1)} all-gather(f32[1,4,1024]{2,1,0:T(4,128)S(1)} %maximum_bitcast_fusion), channel_id=2, replica_groups=mesh['seq_0'=4,'seq_1'=16,'seq_2'=2,'head'=4] {'seq_2'}, dimensions={0}, use_global_device_ids=true | all-gather | bytes 49152 | tf_op jit(solution)/shard_map/all_gather | solution.py:31
  29.6 24.2 %all-gather.4 = f32[16,4,1024]{2,1,0:T(4,128)S(1)} all-gather(f32[1,4,1024]{2,1,0:T(4,128)S(1)} %maximum_bitcast_fusion.1), channel_id=3, replica_groups=mesh['seq_0'=4,'seq_1'=16,'seq_2'=2,'head'=4] {'seq_1'}, dimensions={0}, use_global_device_ids=true | all-gather | bytes 278528 | tf_op jit(solution)/shard_map/all_gather | solution.py:31
  86.4 5.0 %multiply_bitcast_fusion = (f32[1,2,8,128]{3,1,2,0:T(2,128)S(1)}, f32[1,2,1024]{2,1,0:T(2,128)S(1)}) fusion(f32[]{:T(128)} %bitcast.51, f32[]{:T(128)} %bitcast.59, f32[16,4,1024]{2,1,0:T(4,128)S(1)} %all-gather.4, f32[]{:T(128)} %bitcast.58, f32[]{:T(128)} %bitcast.57, f32[]{:T(128)} %bitcast.56, f32[]{:T(128)} %bitcast.55, f32[]{:T(128)} %bitcast.54, ...), kind=kLoop, calls=%fused_computation.156 | loop fusion | flops 32768 | bytes 81956
  91.4 5.0 %bitcast_add_fusion.17 = f32[2,1024]{1,0:T(2,128)S(1)} fusion(f32[16,4,1024]{2,1,0:T(4,128)S(1)} %all-gather.4, f32[]{:T(128)} %bitcast.37, f32[]{:T(128)} %bitcast.39, f32[]{:T(128)} %bitcast.41, f32[]{:T(128)} %bitcast.43, f32[]{:T(128)} %bitcast.45, f32[]{:T(128)} %bitcast.47, f32[]{:T(128)} %bitcast.49, f32[1,2,1024]{2,1,0:T(2,128)S(1)} %get-tuple-element.309, ...), kind=kLoop, calls=%fused_computation.132 | loop fusion | flops 32768 | bytes 81952 | tf_op jit(solution)/shard_map/add | solution.py:100
  96.4 9.3 %all-gather.5 = f32[4,4,1024]{2,1,0:T(4,128)S(1)} all-gather(f32[1,4,1024]{2,1,0:T(4,128)S(1)} %maximum_bitcast_fusion.2), channel_id=4, replica_groups=mesh['seq_0'=4,'seq_1'=16,'seq_2'=2,'head'=4] {'seq_0'}, dimensions={0}, use_global_device_ids=true | all-gather | bytes 81920 | tf_op jit(solution)/shard_map/all_gather | solution.py:31
  112.3 10.0 %bitcast_add_fusion.9 = (f32[2,1024]{1,0:T(2,128)S(1)}, f32[1,2,1024]{2,1,0:T(2,128)S(1)}, f32[1,2,1024]{2,1,0:T(2,128)S(1)}) fusion(f32[2,1024]{1,0:T(2,128)S(1)} %get-tuple-element.373, f32[2,1024]{1,0:T(2,128)S(1)} %bitcast_add_fusion.17, pred[]{:T(512)} %gt.89, pred[]{:T(512)} %gt.88, pred[]{:T(512)} %gt.87, pred[]{:T(512)} %gt.86, pred[]{:T(512)} %gt.85, ...), kind=kLoop, calls=%fused_computation.117 | loop fusion | flops 124928 | bytes 204906 | tf_op jit(solution)/shard_map/add | solution.py:100
  123.8 11.8 %collective-permute-start.1 = (bf16[256]{0:T(256)(128)(2,1)S(1)}, bf16[256]{0:T(256)(128)(2,1)S(1)}, u32[]{:S(2)}, u32[]{:S(2)}) collective-permute-start(bf16[256]{0:T(256)(128)(2,1)S(1)} %slice_convert_fusion), channel_id=1, source_target_pairs={{0,4},{4,8},{8,12},{12,16},{16,20},{20,24},{24,28},{28,32},{32,36}... | collective-permute-start | bytes 1544 | tf_op jit(solution)/shard_map/ppermute | solution.py:81
  136.4 1.9 collective-permute-start
  139.1 3.0 collective-permute-start.2
  142.8 82.6 %all-gather.7 = f32[128,4,2]{1,2,0:T(2,128)S(1)} all-gather(f32[1,4,2]{1,2,0:T(2,128)S(1)} %maximum_bitcast_fusion.4), channel_id=1, replica_groups=mesh['seq_0'=4,'seq_1'=16,'seq_2'=2,'head'=4] {'seq_0','seq_1','seq_2'}, dimensions={0}, use_global_device_ids=true | all-gather | bytes 4128 | tf_op jit(solution)/shard_map/all_gather | solution.py:68
  225.7 4.3 %divide_bitcast_fusion = (f32[8,2,128]{2,0,1:T(8,128)S(1)}, f32[2,8,128]{2,1,0:T(8,128)S(1)}) fusion(f32[]{:T(128)S(6)} %max.56, f32[1,2,8,128]{3,1,2,0:T(2,128)S(1)} %bitcast.436, f32[1,2,8,128]{3,1,2,0:T(2,128)S(1)} %bitcast.435, pred[]{:T(512)} %gt.89, pred[]{:T(512)} %gt.88, pred[]{:T(512)} %gt.87, pred[]{:T(512)} %gt.86, pred[]{:T(512)} %gt.85, ...), kind=kLoop, calls=%fused_computation.136 | loop fusion | flops 55296 | bytes 114732 | tf_op jit(solution)/shard_map/transpose | solution.py:198
  234.1 2.3 pad_maximum_fusion.1
  236.5 2.3 pad_maximum_fusion
  241.4 28.9 %all-gather.10.cloned.1.call-done = bf16[128,4,2048]{2,1,0:T(4,128)(2,1)} async-done(((bf16[1,4,2048]{2,1,0:T(4,128)(2,1)}), bf16[128,4,2048]{2,1,0:T(4,128)(2,1)}) %all-gather.10.cloned.1.call-update) | async-done | bytes 2097168 | tf_op jit(solution)/shard_map/all_gather | solution.py:61
  270.3 2.5 reshape.645
  274.1 2.4 copy.106
  277.8 62.7 %while.12 = (s32[]{:T(128)}, f32[8,512,128]{2,1,0:T(8,128)S(1)}, bf16[8,512,128]{1,2,0:T(8,128)(2,1)}, bf16[8,768,128]{1,2,0:T(8,128)(2,1)}, bf16[8,512,128]{1,2...) while((s32[]{:T(128)}, f32[8,512,128]{2,1,0:T(8,128)S(1)}, ...), condition=%wide.region_9.10_spmd.clone.clone, body=%wide.region_3.9_spmd.clone.clone.sunk | while | flops 343215616 | bytes 10306749 | solution.py:251
  287.0 1.7 fusion.125
  294.8 1.7 fusion.125
  310.5 1.7 fusion.125
  318.3 1.7 fusion.125
  334.0 1.7 fusion.125
  340.7 8.0 %all_to_all.6 = f32[4,1,512]{2,1,0:T(1,128)S(1)} all-to-all(f32[4,1,512]{2,1,0:T(1,128)S(1)} %broadcast_in_dim.159), channel_id=1, replica_groups=mesh['seq_0'=4,'seq_1'=16,'seq_2'=2,'head'=4] {'head'}, dimensions={0} | all-to-all | bytes 16384 | tf_op jit(solution)/shard_map/all_to_all | solution.py:86
  (203 shorter events, 78.0 us)
Async XLA Ops:
  6.5 6.7 %copy-start.1 = (bf16[512,1024]{1,0:T(8,128)(2,1)S(1)}, bf16[512,1024]{1,0:T(8,128)(2,1)}, u32[]{:S(2)}) copy-start(bf16[512,1024]{1,0:T(8,128)(2,1)} %param.10) | copy-start | bytes 3145732
  6.5 263.8 %all-gather.10.cloned.1.call-start = ((), (), s32[]{:S(2)}) async-start(), calls=%async_computation.1 | async-start | bytes 2113536 | tf_op jit(solution)/shard_map/all_gather | solution.py:61
  122.7 107.4 %copy-start.2 = (s32[512]{0:T(512)S(1)}, s32[512]{0:T(512)}, u32[]{:S(2)}) copy-start(s32[512]{0:T(512)} %param.12) | copy-start | bytes 6148
  123.8 109.0 %collective-permute-start.1 = (bf16[256]{0:T(256)(128)(2,1)S(1)}, bf16[256]{0:T(256)(128)(2,1)S(1)}, u32[]{:S(2)}, u32[]{:S(2)}) collective-permute-start(bf16[256]{0:T(256)(128)(2,1)S(1)} %slice_convert_fusion), channel_id=1, source_target_pairs={{0,4},{4,8},{8,12},{12,16},{16,20},{20,24},{24,28},{28,32},{32,36}... | collective-permute-start | bytes 1544 | tf_op jit(solution)/shard_map/ppermute | solution.py:81
  136.4 100.1 %collective-permute-start = (bf16[256,1024]{0,1:T(8,128)(2,1)}, bf16[256,1024]{0,1:T(8,128)(2,1)}, u32[]{:S(2)}, u32[]{:S(2)}) collective-permute-start(bf16[256,1024]{0,1:T(8,128)(2,1)} %slice.471), channel_id=1, source_target_pairs={{0,4},{4,8},{8,12},{12,16},{16,20},{20,24},{24,28},{28,32},{32,36}... | collective-permute-start | bytes 1572872 | tf_op jit(solution)/shard_map/ppermute | solution.py:81
  139.1 95.0 %collective-permute-start.2 = (bf16[256,1024]{0,1:T(8,128)(2,1)}, bf16[256,1024]{0,1:T(8,128)(2,1)}, u32[]{:S(2)}, u32[]{:S(2)}) collective-permute-start(bf16[256,1024]{0,1:T(8,128)(2,1)} %slice.546), channel_id=1, source_target_pairs={{0,4},{4,8},{8,12},{12,16},{16,20},{20,24},{24,28},{28,32},{32,36}... | collective-permute-start | bytes 1572872 | tf_op jit(solution)/shard_map/ppermute | solution.py:81
  274.1 3.7 %copy-start = (f32[8,512,128]{2,1,0:T(8,128)S(1)}, f32[8,512,128]{2,1,0:T(8,128)}, u32[]{:S(2)}) copy-start(f32[8,512,128]{2,1,0:T(8,128)} %custom-call) | copy-start | bytes 6291460
  340.5 8.3 %copy-start.3 = (f32[1024]{0:T(1024)S(1)}, f32[1024]{0:T(1024)}, u32[]{:S(2)}) copy-start(f32[1024]{0:T(1024)} %param.13) | copy-start | bytes 12292
Sparse Core Ops, SparseCore 0:
  123.9 146.3 all-gather.9
where the time goes:
time: 359 us; the launch traced here: 357 us
  blocking collectives  132 us (37%)
  between operations  55.7 us (16%)
  matrix products  50.9 us (14%)
  other arithmetic  43.5 us (12%)
  waiting for transfers between devices  29 us (8%)
  local copies, waits for them, and re-layouts  28 us (8%)
  starting transfers between devices  16.7 us (5%)
    all_gather x1, blocking collectives, rows_first(): out = lax.all_gather(both, axis, axis=0, tiled=True)  82.6 us
    all_gather x3, blocking collectives, all_in_one(): both, at, found = (lax.all_gather(jnp.concatenate(lines), axis), 0, {})  41.9 us
    all_gather x1, waiting for transfers between devices, side_by_side(): lax.all_gather(both, axis, axis=dim, tiled=True)  28.9 us
    ppermute x3, starting transfers between devices, shifted(): return lax.ppermute(block, axis, route)  16.7 us
    add x2, other arithmetic, tail_combine(): late_sum + late_all * early_sum  15 us
    dot_general x8, matrix products, per_head(): jnp.einsum('td,sd->ts', head_query, head_key, preferred_element_type=jnp....  13.9 us
    dot_general x8, matrix products, per_head(): jnp.einsum('ts,sd->td', win_weight.astype(jnp.bfloat16), head_value, pref...  11.3 us
    dot_general x8, matrix products, per_head(): jnp.einsum('td,sd->ts', head_query, land_key, preferred_element_type=jnp....  10.9 us
  transfers between devices with their start and end apart: 4, of which 1 were waited for; matrix products, arithmetic and copies ran while one was open for 5% of the time, Pallas kernels for 0%

commit v1 on v0

v1 whole, which is shorter than its diff:
```python
import functools
import jax
import jax.numpy as jnp
from jax import lax
from jax.experimental import pallas as pl
from jax.experimental.pallas import tpu as pltpu
from jax.sharding import PartitionSpec as P

HEADS = 32
HD = 128
CAP = 4
BLK = 128
SCALE = 1.0 / HD**0.5
LOG2E = 1.4426950408889634
EXP_SCALE = SCALE * LOG2E
NEG = -1e30
EPS = 1e-6
NX, NZ, NC = 4, 16, 2
MESH = pl.DeviceIdType.MESH
F32 = jnp.float32
BF16 = jnp.bfloat16
NT = (((1,), (1,)), ((), ()))


def dot(a, b):
    return jnp.dot(a, b, preferred_element_type=F32)


def dot_nt(a, b):
    return lax.dot_general(a, b, NT, preferred_element_type=F32)


def iota(shape, dim):
    return lax.broadcasted_iota(jnp.int32, shape, dim)


def kernel(
    dims,
    q_hbm, k_hbm, v_hbm, scales, seg_ref, gain_ref,
    out_ref,
    raw_q, raw_k, raw_v, qd, kx, vx,
    packet, pbuf, lmk, lkf, lvf, tab, kaux, qaux, ekh, ekl, evv, lbias,
    maskb, acc, mrow, squares, ssbuf,
    in_sem, halo_s, halo_r, ps, pr, zs, zr, xs, xr, ds, dr, ys, yr,
):
    nx, nz, ny = dims
    pairs = nz // 2
    ndev = nx * nz * NC
    tok, width = out_ref.shape
    half = tok // 2
    heads = width // HD
    d = lax.axis_index("seq")
    y = lax.axis_index("head")
    core = lax.rem(d, 2)
    zpos = lax.rem(lax.div(d, 2), nz)
    xpos = lax.div(d, 2 * nz)
    pair = lax.div(zpos, 2)
    group = lax.div(d, 4)
    ngroups = ndev // 4
    member = lax.rem(d, 4)
    sgn = 1 - 2 * core
    partner = d + sgn

    def at(x, z, c):
        return (x * nz + z) * 2 + c

    loads = [
        pltpu.make_async_copy(src, dst, in_sem.at[n])
        for n, (src, dst) in enumerate(((k_hbm, raw_k), (v_hbm, raw_v), (q_hbm, raw_q)))
    ]
    for load in loads:
        load.start()

    znext = lax.rem(zpos + 2 * sgn + nz, nz)
    zprev = lax.rem(zpos - 2 * sgn + nz, nz)
    peers = [group * 4 + lax.rem(member + n, 4) for n in (1, 2, 3)]
    nextg = [lax.rem(group + 1, ngroups) * 4 + n for n in range(4)]
    prevg = [lax.rem(group + ngroups - 1, ngroups) * 4 + n for n in range(4)]
    xpeers = [at(lax.rem(xpos + n, nx), zpos, core) for n in range(1, nx)]
    zpeers = [at(xpos, znext, core), at(xpos, zprev, core)]
    ypeers = [lax.rem(y + n, ny) for n in range(1, ny)]
    barrier = pltpu.get_barrier_semaphore()
    greeted = peers + nextg + prevg + xpeers + zpeers
    for peer in greeted:
        pl.semaphore_signal(barrier, inc=1, device_id={"seq": peer}, device_id_type=MESH)
    for peer in ypeers:
        pl.semaphore_signal(barrier, inc=1, device_id={"head": peer}, device_id_type=MESH)

    seg = seg_ref[...]
    first = jnp.min(seg, axis=1, keepdims=True)
    last = jnp.max(seg, axis=1, keepdims=True)
    end = last - first
    local = seg - first
    endf = end.astype(F32)
    row = iota((16, tok), 0)
    pos = iota((16, tok), 1)
    slot = lax.rem(row, 4)
    wide = jnp.broadcast_to(local, (16, tok))
    is_slot = (row < 8) & (wide == slot) & (slot < end)
    is_tail = (row >= 8) & (wide == end) & (lax.rem(row, 2) == lax.div(pos, half))
    pick32 = jnp.where(is_slot | is_tail, 1.0, 0.0)
    pick = pick32.astype(BF16)
    counts = jnp.sum(pick32, axis=1, keepdims=True)
    r16 = iota((16, HD), 0)
    l16 = iota((16, HD), 1)
    want = jnp.where(r16 < 4, r16, jnp.where((r16 >= 8) & (r16 < 10), r16 - 4, -1))
    count_row = jnp.sum(jnp.where(l16 == want, counts, 0.0), axis=0, keepdims=True)
    lane = iota((1, HD), 1)
    count_row = jnp.where(lane == 6, endf, count_row)
    count_wide = jnp.concatenate([count_row] + [jnp.zeros((1, HD), F32)] * (heads - 1), axis=1)

    def dequantize(src, which, dst, base):
        def block(b, _):
            for h in range(heads):
                factor = scales[which, b, h]
                rows = pl.ds(pl.multiple_of(b * BLK, BLK), BLK)
                piece = src[rows, h * HD : (h + 1) * HD].astype(F32) * factor
                dst[pl.ds(pl.multiple_of(base + b * BLK, BLK), BLK), h * HD : (h + 1) * HD] = (
                    piece.astype(BF16)
                )
            return 0

        lax.fori_loop(0, tok // BLK, block, 0)

    loads[0].wait()
    dequantize(raw_k, 1, kx, half)
    key_sums = dot(pick, kx[half:, :])
    loads[1].wait()
    dequantize(raw_v, 2, vx, half)
    value_sums = dot(pick, vx[half:, :])
    r8 = iota((8, width), 0)
    packet[0] = jnp.where(r8 < 4, key_sums[0:8], value_sums[0:8])
    packet[1] = jnp.where(
        r8 < 2, key_sums[8:16], jnp.where(r8 == 4, count_wide, value_sums[8:16])
    )

    pl.semaphore_wait(barrier, len(greeted) + len(ypeers))

    sends = []
    for n, peer in enumerate(peers):
        sends.append(
            pltpu.make_async_remote_copy(
                src_ref=packet, dst_ref=pbuf.at[1 + member], send_sem=ps.at[n],
                recv_sem=pr.at[1 + member], device_id={"seq": peer}, device_id_type=MESH,
            )
        )
    for copy in sends:
        copy.start()

    def tail_copy(n):
        return pltpu.make_async_remote_copy(
            src_ref=packet.at[1], dst_ref=pbuf.at[0, 1], send_sem=ps.at[3 + n],
            recv_sem=pr.at[0], device_id={"seq": nextg[n]}, device_id_type=MESH,
        )

    sends_on = (member == 3) & (group < ngroups - 1)

    @pl.when(sends_on)
    def _():
        for n in range(4):
            tail_copy(n).start()

    follower = lax.rem(d + 1, ndev)

    def halo_copy(n, ref):
        return pltpu.make_async_remote_copy(
            src_ref=ref.at[pl.ds(tok, half)], dst_ref=ref.at[pl.ds(0, half)],
            send_sem=halo_s.at[n], recv_sem=halo_r.at[n],
            device_id={"seq": follower}, device_id_type=MESH,
        )

    @pl.when(d < ndev - 1)
    def _():
        halo_copy(0, kx).start()
        halo_copy(1, vx).start()

    @pl.when(d == 0)
    def _():
        kx[0:half, :] = jnp.zeros((half, width), BF16)
        vx[0:half, :] = jnp.zeros((half, width), BF16)

    @pl.when(group == 0)
    def _():
        pbuf[0, 1] = jnp.zeros((8, width), F32)

    for r in range(1, nx):
        @pl.when(xpos < r)
        def _():
            tab[r * pairs : (r + 1) * pairs] = jnp.zeros((pairs, 16, tab.shape[2]), BF16)

    pbuf[1 + member] = packet[...]
    for n in (1, 2, 3):
        other = lax.rem(member + n, 4)
        pltpu.make_async_remote_copy(
            src_ref=packet, dst_ref=pbuf.at[1 + other], send_sem=ps.at[0],
            recv_sem=pr.at[1 + other], device_id={"seq": peers[0]}, device_id_type=MESH,
        ).wait_recv()

    @pl.when(group > 0)
    def _():
        tail_copy(0).wait_recv()

    lead = group == 0
    r8n = iota((8, HD), 0)
    l8n = iota((8, HD), 1)
    tails = [pbuf[n, 1] for n in range(5)]

    def whole_tail(t):
        return t[0:1] + t[1:2], t[2:3] + t[3:4], t[4:5, 4:5] + t[4:5, 5:6]

    for j in range(4):
        key_tail, value_tail, tail_count = whole_tail(tails[j])
        for back in range(1, j):
            extra = whole_tail(tails[j - back])
            key_tail = key_tail + jnp.where(lead, extra[0], 0.0)
            value_tail = value_tail + jnp.where(lead, extra[1], 0.0)
            tail_count = tail_count + jnp.where(lead, extra[2], 0.0)
        total = pbuf[1 + j, 0]
        total = total + jnp.where(r8 == 0, key_tail, jnp.where(r8 == 4, value_tail, 0.0))
        crow = tails[j + 1][4:5, 0:HD]
        slot8 = lax.rem(r8n, 4)
        number = jnp.sum(jnp.where(l8n == slot8, crow, 0.0), axis=1, keepdims=True)
        rc = iota((8, 1), 0)
        number = number + jnp.where(lax.rem(rc, 4) == 0, tail_count, 0.0)
        number = jnp.maximum(number, 1.0)
        done = (lax.rem(rc, 4)).astype(F32) < crow[0:1, 6:7]
        value = total / number
        lmk[...] = value
        lkf[4 * j : 4 * j + 4, :] = lmk[0:4, :]
        lvf[4 * j : 4 * j + 4, :] = lmk[4:8, :]
        bias = jnp.where(done, jnp.log(number) * (1.0 / SCALE), NEG)
        lbias[4 * j : 4 * j + 4, :] = jnp.broadcast_to(bias, (8, HD))[0:4]

    own_bias = lbias[...]
    hi = own_bias.astype(BF16).astype(F32)
    mid = (own_bias - hi).astype(BF16).astype(F32)
    low = own_bias - hi - mid
    aux = jnp.where(l16 == 0, hi, jnp.where(l16 == 1, mid, jnp.where(l16 == 2, low, 0.0)))
    own_keys = lkf[...].astype(BF16)
    own_values = lvf[...].astype(BF16)
    tab[group, :, 0:width] = own_keys
    tab[group, :, width : 2 * width] = own_values
    tab[group, :, 2 * width :] = aux.astype(BF16)

    def chunk_copy(row_x, p, send_sem, recv_sem, target):
        g = row_x * pairs + p
        return pltpu.make_async_remote_copy(
            src_ref=tab.at[g], dst_ref=tab.at[g], send_sem=send_sem, recv_sem=recv_sem,
            device_id={"seq": target}, device_id_type=MESH,
        )

    def ring_pair(i, c_sgn):
        return lax.rem(pair - c_sgn * i + 2 * pairs, pairs)

    steps = pairs // 2

    def ring_send(i):
        return chunk_copy(xpos, ring_pair(i - 1, sgn), zs.at[i - 1], zr.at[i - 1],
                          at(xpos, znext, core))

    def ring_recv(i):
        return chunk_copy(xpos, ring_pair(i, sgn), zs.at[i - 1], zr.at[i - 1],
                          at(xpos, znext, core))

    def row_send(dx, i):
        return chunk_copy(xpos, ring_pair(i, sgn), xs.at[dx - 1, i], xr.at[dx - 1, i],
                          at(lax.rem(xpos + dx, nx), zpos, core))

    def row_recv(dx, i):
        return chunk_copy(xpos - dx, ring_pair(i, sgn), xs.at[dx - 1, i], xr.at[dx - 1, i],
                          at(lax.rem(xpos + dx, nx), zpos, core))

    def pass_on(dx, i):
        return chunk_copy(xpos - dx, ring_pair(i, sgn), ds.at[dx, i], dr.at[dx, i], partner)

    def passed(dx, i):
        return chunk_copy(xpos - dx, ring_pair(i, -sgn), ds.at[dx, i], dr.at[dx, i], partner)

    def if_core0(i, extra=None):
        conds = []
        if i == 0 or i == steps:
            conds.append(core == 0)
        if extra is not None:
            conds.append(extra)
        return functools.reduce(jnp.logical_and, conds) if conds else None

    def if_core1_partner(i, extra=None):
        conds = []
        if i == 0 or i == steps:
            conds.append(core == 1)
        if extra is not None:
            conds.append(extra)
        return functools.reduce(jnp.logical_and, conds) if conds else None

    def run_if(cond, fn):
        if cond is None:
            fn()
        else:
            pl.when(cond)(fn)

    def ring_start(i):
        run_if(if_core0(i), lambda: ring_send(i).start())

    def row_start(i):
        for dx in range(1, nx):
            run_if(if_core0(i, xpos + dx < nx), lambda: row_send(dx, i).start())

    ring_start(1)
    row_start(0)

    before = pbuf[member, 1]
    one_back = pbuf[jnp.maximum(member - 1, 0), 1]
    two_back = pbuf[jnp.maximum(member - 2, 0), 1]
    ext2 = lead & (member >= 2)
    ext3 = lead & (member == 3)

    def extra_tail(r0, c0):
        value2 = one_back[r0 : r0 + 1] + one_back[r0 + 1 : r0 + 2]
        value3 = two_back[r0 : r0 + 1] + two_back[r0 + 1 : r0 + 2]
        return jnp.where(ext2, value2, 0.0) + jnp.where(ext3, value3, 0.0)

    extra_count = jnp.where(ext2, one_back[4:5, 4:5] + one_back[4:5, 5:6], 0.0) + jnp.where(
        ext3, two_back[4:5, 4:5] + two_back[4:5, 5:6], 0.0
    )
    prev_count = before[4:5, 5:6]
    early_count = before[4:5, 4:5] + extra_count
    late_count = early_count + prev_count
    early_size = jnp.maximum(early_count, 1.0)
    late_size = jnp.maximum(late_count, 1.0)
    early_key = before[0:1] + extra_tail(0, 0)
    late_key = (early_key + before[1:2]) / late_size
    early_key = early_key / early_size
    early_value = before[2:3] + extra_tail(2, 0)
    late_value = (early_value + before[3:4]) / late_size
    early_value = early_value / early_size
    rw = iota((16, width), 0)
    run_keys = jnp.where(rw == 0, early_key, jnp.where(rw == 1, late_key, 0.0))
    run_hi = run_keys.astype(BF16)
    run_lo = (run_keys - run_hi.astype(F32)).astype(BF16)
    run_values = jnp.where(rw == 0, early_value, jnp.where(rw == 1, late_value, 0.0))
    ekh[0:16, :] = own_keys
    ekh[16:32, :] = run_hi
    ekh[32:, :] = jnp.zeros((HD - 32, width), BF16)
    ekl[0:16, :] = jnp.zeros((16, width), BF16)
    ekl[16:32, :] = run_lo
    ekl[32:, :] = jnp.zeros((HD - 32, width), BF16)
    evv[0:16, :] = own_values
    evv[16:32, :] = run_values.astype(BF16)
    evv[32:, :] = jnp.zeros((HD - 32, width), BF16)

    columns = jnp.broadcast_to(local.astype(F32), (HD, tok)).T
    own_row = jnp.sum(jnp.where(l16 == r16, own_bias, 0.0), axis=0, keepdims=True)
    early_bias = jnp.where(early_count > 0.5, jnp.log(early_size) * (1.0 / SCALE), NEG)
    late_bias = jnp.where(late_count > 0.5, jnp.log(late_size) * (1.0 / SCALE), NEG)
    key_row = jnp.concatenate(
        [jnp.where(iota((1, half), 1).astype(F32) >= half - prev_count, 0.0, -1.0),
         local.astype(F32)], axis=1,
    )
    el = iota((half, HD), 1)
    owner = lax.div(el, 4)
    for b in range(2):
        mine = columns[b * half : (b + 1) * half]
        wide_mine = jnp.concatenate([mine] * (tok // HD), axis=1)
        keys = key_row[:, b * half : b * half + tok]
        i_pos = iota((half, tok), 0) + half
        j_pos = iota((half, tok), 1)
        ok = (wide_mine == keys) & (j_pos <= i_pos)
        maskb[b, :, 0:tok] = jnp.where(ok, 0.0, NEG)
        visible = (el < 16) & (
            (owner < member) | ((owner == member) & (lax.rem(el, 4).astype(F32) < mine))
        )
        run_bias = early_bias if b == 0 else late_bias
        run_ok = (el == 16 + b) & (mine == 0.0)
        maskb[b, :, tok:] = jnp.where(visible, own_row, jnp.where(run_ok, run_bias, NEG))
    qaux[...] = jnp.where(iota((half, HD), 1) < 3, 1.0, 0.0).astype(BF16)
    loads[2].wait()
    dequantize(raw_q, 0, qd, 0)

    ones_tok = jnp.ones((tok, HD), BF16)
    ones_ext = jnp.ones((HD, HD), BF16)

    def window(h, b):
        lanes = pl.ds(pl.multiple_of(h * HD, HD), HD)
        q = qd[b * half : (b + 1) * half, lanes]
        keys = kx[b * half : b * half + tok, lanes]
        ext = jnp.concatenate([ekh[:, lanes], ekl[:, lanes]], axis=1)
        s = jnp.concatenate(
            [dot_nt(q, keys), dot_nt(jnp.concatenate([q, q], axis=1), ext)], axis=1
        ) + maskb[b]
        m = jnp.max(s, axis=1, keepdims=True)
        p = jnp.exp2((s - m) * EXP_SCALE).astype(BF16)
        v = jnp.concatenate([vx[b * half : b * half + tok, lanes], ones_tok], axis=1)
        ev = jnp.concatenate([evv[:, lanes], ones_ext], axis=1)
        acc[h, b * half : (b + 1) * half, :] = dot(p[:, :tok], v) + dot(p[:, tok:], ev)
        mrow[h, b * half : (b + 1) * half, :] = jnp.broadcast_to(m, (half, HD))

    def windows(lo, hi, b):
        def body(h, _):
            window(h, b)
            return 0

        lax.fori_loop(lo, hi, body, 0)

    share = heads // steps

    def landed(i):
        def go():
            ring_recv(i).wait_recv()
            if i < steps:
                ring_start(i + 1)

        run_if(if_core0(i), go)
        row_start(i)
        run_if(if_core0(i), lambda: pass_on(0, i).start())

    for i in range(1, steps + 1):
        landed(i)
        windows((i - 1) * share, i * share, 1)

    def rows_landed(i):
        for dx in range(1, nx):
            def go():
                row_recv(dx, i).wait_recv()
                pass_on(dx, i).start()

            run_if(if_core0(i, xpos >= dx), go)

    for i in range(0, steps - 1):
        rows_landed(i)

    @pl.when(d > 0)
    def _():
        halo_copy(0, kx).wait_recv()
        halo_copy(1, vx).wait_recv()

    windows(0, heads // 2, 0)
    for i in range(steps - 1, steps + 1):
        rows_landed(i)
    windows(heads // 2, heads, 0)
    for dx in range(nx):
        for i in range(0 if dx else 1, steps + 1):
            run_if(
                if_core1_partner(i, (xpos >= dx) if dx else None),
                lambda: passed(dx, i).wait_recv(),
            )

    nkeys = ngroups * 16
    flat_aux = tab[:, :, 2 * width :].reshape(nkeys, HD)
    key_group = lax.div(iota((nkeys, HD), 0), 16)
    off = jnp.where(iota((nkeys, HD), 1) == 0, NEG, 0.0)
    kaux[...] = jnp.where(key_group < group, flat_aux.astype(F32), off).astype(BF16)
    squares[...] = jnp.zeros(squares.shape, F32)
    ones_key = jnp.ones((nkeys, HD), BF16)

    def landmarks(h, _):
        lanes = pl.ds(pl.multiple_of(h * HD, HD), HD)
        vlanes = pl.ds(pl.multiple_of(width + h * HD, HD), HD)
        keys = jnp.concatenate([tab[:, :, lanes].reshape(nkeys, HD), kaux[...]], axis=1)
        values = jnp.concatenate([tab[:, :, vlanes].reshape(nkeys, HD), ones_key], axis=1)
        for b in range(2):
            rows = slice(b * half, (b + 1) * half)
            q = jnp.concatenate([qd[rows, lanes], qaux[...]], axis=1)
            s = dot_nt(q, keys)
            old = mrow[h, rows, :]
            m = jnp.maximum(old, jnp.max(s, axis=1, keepdims=True))
            fade = jnp.exp2((old - m) * EXP_SCALE)
            p = jnp.exp2((s - jnp.concatenate([m] * (nkeys // HD), axis=1)) * EXP_SCALE)
            o = dot(p.astype(BF16), values)
            prior = acc[h, rows, :]
            top = prior[:, :HD] * fade + o[:, :HD]
            bottom = prior[:, HD:] * fade + o[:, HD:]
            a = top / bottom
            acc[h, rows, 0:HD] = a
            squares[rows, :] += a * a
        return 0

    lax.fori_loop(0, heads, landmarks, 0)

    ssbuf[0] = jnp.broadcast_to(jnp.sum(squares[...].T, axis=0, keepdims=True), (8, tok))

    def square_copy(n):
        return pltpu.make_async_remote_copy(
            src_ref=ssbuf.at[0], dst_ref=ssbuf.at[n + 1], send_sem=ys.at[n],
            recv_sem=yr.at[n], device_id={"head": ypeers[n]}, device_id_type=MESH,
        )

    for n in range(ny - 1):
        square_copy(n).start()
    for n in range(ny - 1):
        square_copy(n).wait_recv()
    total = ssbuf[0, 0:1]
    for n in range(1, ny):
        total = total + ssbuf[n, 0:1]
    norm = lax.rsqrt(total / (heads * ny * HD) + EPS)
    norm = jnp.broadcast_to(norm, (HD, tok)).T
    for h in range(heads):
        out_ref[:, h * HD : (h + 1) * HD] = (
            acc[h, :, 0:HD] * norm * gain_ref[:, h * HD : (h + 1) * HD]
        ).astype(BF16)

    for copy in sends:
        copy.wait_send()

    @pl.when(sends_on)
    def _():
        for n in range(4):
            tail_copy(n).wait_send()

    @pl.when(d < ndev - 1)
    def _():
        halo_copy(0, kx).wait_send()
        halo_copy(1, vx).wait_send()

    for i in range(1, steps + 1):
        run_if(if_core0(i), lambda: ring_send(i).wait_send())
    for i in range(0, steps + 1):
        for dx in range(1, nx):
            run_if(if_core0(i, xpos + dx < nx), lambda: row_send(dx, i).wait_send())
        for dx in range(nx):
            if dx or i:
                run_if(
                    if_core0(i, (xpos >= dx) if dx else None),
                    lambda: pass_on(dx, i).wait_send(),
                )
    for n in range(ny - 1):
        square_copy(n).wait_send()


def solution(mesh, nx=NX, nz=NZ):
    ny = mesh.shape["head"]

    def on_device(q_raw, k_raw, v_raw, block_scales, segment_ids, norm_gain):
        tok, width = q_raw.shape
        heads = width // HD
        half = tok // 2
        groups = nx * nz // 2
        steps = nz // 4
        dma = pltpu.SemaphoreType.DMA
        hbm = pl.BlockSpec(memory_space=pl.ANY)
        vmem = pl.BlockSpec(memory_space=pltpu.VMEM)
        smem = pl.BlockSpec(memory_space=pltpu.SMEM)
        return pl.pallas_call(
            functools.partial(kernel, (nx, nz, ny)),
            out_shape=jax.ShapeDtypeStruct((tok, width), BF16),
            in_specs=[hbm, hbm, hbm, smem, vmem, vmem],
            out_specs=vmem,
            scratch_shapes=[
                pltpu.VMEM((tok, width), BF16),
                pltpu.VMEM((tok, width), BF16),
                pltpu.VMEM((tok, width), BF16),
                pltpu.VMEM((tok, width), BF16),
                pltpu.VMEM((tok + half, width), BF16),
                pltpu.VMEM((tok + half, width), BF16),
                pltpu.VMEM((2, 8, width), F32),
                pltpu.VMEM((5, 2, 8, width), F32),
                pltpu.VMEM((8, width), F32),
                pltpu.VMEM((16, width), F32),
                pltpu.VMEM((16, width), F32),
                pltpu.VMEM((groups, 16, 2 * width + HD), BF16),
                pltpu.VMEM((groups * 16, HD), BF16),
                pltpu.VMEM((half, HD), BF16),
                pltpu.VMEM((HD, width), BF16),
                pltpu.VMEM((HD, width), BF16),
                pltpu.VMEM((HD, width), BF16),
                pltpu.VMEM((16, HD), F32),
                pltpu.VMEM((2, half, tok + HD), F32),
                pltpu.VMEM((heads, tok, 2 * HD), F32),
                pltpu.VMEM((heads, tok, HD), F32),
                pltpu.VMEM((tok, HD), F32),
                pltpu.VMEM((ny, 8, tok), F32),
                dma((3,)), dma((2,)), dma((2,)), dma((7,)), dma((5,)),
                dma((steps,)), dma((steps,)),
                dma((nx - 1, steps + 1)), dma((nx - 1, steps + 1)),
                dma((nx, steps + 1)), dma((nx, steps + 1)),
                dma((max(ny - 1, 1),)), dma((max(ny - 1, 1),)),
            ],
            compiler_params=pltpu.CompilerParams(
                collective_id=0, has_side_effects=True, vmem_limit_bytes=60000000
            ),
            name="attention",
        )(
            q_raw, k_raw, v_raw, block_scales,
            segment_ids.reshape(1, tok), norm_gain.reshape(1, width),
        )

    in_specs = (
        P("seq", "head"),
        P("seq", "head"),
        P("seq", "head"),
        P(None, "seq", "head"),
        P("seq"),
        P("head"),
    )
    return jax.shard_map(
        on_device, mesh=mesh, in_specs=in_specs, out_specs=P("seq", "head"), check_vma=False
    )
```

time: 359 us -> 59.7 us (0.17)
  the two profiles are of different devices: /device:TPU:1 before, /device:TPU:32 now
where the time goes in v1:
time: 59.7 us; the launch traced here: 59.5 us
  Pallas kernels  57.2 us (96%)
  local copies, waits for them, and re-layouts  2.26 us (4%)
    pallas_call x1, Pallas kernels, on_device(): pl.pallas_call(functools.partial(kernel, (nx, nz, ny)), out_shape=jax.Sha...  57.2 us
    unnamed x1, local copies, waits for them, and re-layouts  2.26 us

profile of v1, /device:TPU:32, one launch (start us, length us, event | category | flops | bytes accessed | tf_op | source)
XLA Modules:
  0.0 59.5 jit_solution(14489866092800894679)
XLA Ops:
  0.0 57.2 %attention.1 = bf16[512,1024]{1,0:T(8,128)(2,1)} custom-call(bf16[512,1024]{1,0:T(8,128)(2,1)} %q_hbm.1, bf16[512,1024]{1,0:T(8,128)(2,1)} %k_hbm.1, bf16[512,1024]{1,0:T(8,128)(2,1)} %v_hbm.1, f32[3,4,8]{2,1,0:T(4,128)} %scales.1, s32[1,512]{1,0:T(1,128)} %bitcast.3, f32[1,1024]{1,0:T(1,128)} %bitcast.2), custom_call_target="tpu_custom_call" | custom-call | tf_op jit(solution)/shard_map/attention/pallas_call | solution.py:542
  57.2 2.3 %copy.8 = bf16[512,1024]{1,0:T(8,128)(2,1)} copy(bf16[512,1024]{1,0:T(8,128)(2,1)} %attention.1) | data formatting | bytes 2097152

commit v2 on v1

--- a/solution.py
+++ b/solution.py
@@ -36,7 +36,7 @@
 
 def kernel(
     dims,
-    q_hbm, k_hbm, v_hbm, scales, seg_ref, gain_ref,
+    q_hbm, k_hbm, v_hbm, scales, seg_ref,
     out_ref,
     raw_q, raw_k, raw_v, qd, kx, vx,
     packet, pbuf, lmk, lkf, lvf, tab, kaux, qaux, ekh, ekl, evv, lbias,
@@ -188,6 +188,20 @@
         def _():
             tab[r * pairs : (r + 1) * pairs] = jnp.zeros((pairs, 16, tab.shape[2]), BF16)
 
+    columns = jnp.broadcast_to(local.astype(F32), (HD, tok)).T
+    own_ids = local.astype(F32)
+    for b in range(2):
+        mine = columns[b * half : (b + 1) * half]
+        width_b = half * (b + 1)
+        wide_mine = jnp.concatenate([mine] * (width_b // HD), axis=1)
+        i_pos = iota((half, width_b), 0) + b * half
+        ok = (wide_mine == own_ids[:, :width_b]) & (iota((half, width_b), 1) <= i_pos)
+        start = half * (1 - b)
+        maskb[b, :, start:tok] = jnp.where(ok, 0.0, NEG)
+    qaux[...] = jnp.where(iota((half, HD), 1) < 3, 1.0, 0.0).astype(BF16)
+    loads[2].wait()
+    dequantize(raw_q, 0, qd, 0)
+
     pbuf[1 + member] = packet[...]
     for n in (1, 2, 3):
         other = lax.rem(member + n, 4)
@@ -276,18 +290,18 @@
     def passed(dx, i):
         return chunk_copy(xpos - dx, ring_pair(i, -sgn), ds.at[dx, i], dr.at[dx, i], partner)
 
-    def if_core0(i, extra=None):
+    def here(i, extra=None):
         conds = []
         if i == 0 or i == steps:
-            conds.append(core == 0)
+            conds.append(core == (0 if i == 0 else 1))
         if extra is not None:
             conds.append(extra)
         return functools.reduce(jnp.logical_and, conds) if conds else None
 
-    def if_core1_partner(i, extra=None):
+    def there(i, extra=None):
         conds = []
         if i == 0 or i == steps:
-            conds.append(core == 1)
+            conds.append(core == (1 if i == 0 else 0))
         if extra is not None:
             conds.append(extra)
         return functools.reduce(jnp.logical_and, conds) if conds else None
@@ -299,11 +313,11 @@
             pl.when(cond)(fn)
 
     def ring_start(i):
-        run_if(if_core0(i), lambda: ring_send(i).start())
+        run_if(here(i), lambda: ring_send(i).start())
 
     def row_start(i):
         for dx in range(1, nx):
-            run_if(if_core0(i, xpos + dx < nx), lambda: row_send(dx, i).start())
+            run_if(here(i, xpos + dx < nx), lambda: row_send(dx, i).start())
 
     ring_start(1)
     row_start(0)
@@ -348,58 +362,55 @@
     evv[16:32, :] = run_values.astype(BF16)
     evv[32:, :] = jnp.zeros((HD - 32, width), BF16)
 
-    columns = jnp.broadcast_to(local.astype(F32), (HD, tok)).T
     own_row = jnp.sum(jnp.where(l16 == r16, own_bias, 0.0), axis=0, keepdims=True)
     early_bias = jnp.where(early_count > 0.5, jnp.log(early_size) * (1.0 / SCALE), NEG)
     late_bias = jnp.where(late_count > 0.5, jnp.log(late_size) * (1.0 / SCALE), NEG)
-    key_row = jnp.concatenate(
-        [jnp.where(iota((1, half), 1).astype(F32) >= half - prev_count, 0.0, -1.0),
-         local.astype(F32)], axis=1,
-    )
     el = iota((half, HD), 1)
     owner = lax.div(el, 4)
     for b in range(2):
         mine = columns[b * half : (b + 1) * half]
-        wide_mine = jnp.concatenate([mine] * (tok // HD), axis=1)
-        keys = key_row[:, b * half : b * half + tok]
-        i_pos = iota((half, tok), 0) + half
-        j_pos = iota((half, tok), 1)
-        ok = (wide_mine == keys) & (j_pos <= i_pos)
-        maskb[b, :, 0:tok] = jnp.where(ok, 0.0, NEG)
         visible = (el < 16) & (
             (owner < member) | ((owner == member) & (lax.rem(el, 4).astype(F32) < mine))
         )
         run_bias = early_bias if b == 0 else late_bias
         run_ok = (el == 16 + b) & (mine == 0.0)
         maskb[b, :, tok:] = jnp.where(visible, own_row, jnp.where(run_ok, run_bias, NEG))
-    qaux[...] = jnp.where(iota((half, HD), 1) < 3, 1.0, 0.0).astype(BF16)
-    loads[2].wait()
-    dequantize(raw_q, 0, qd, 0)
+    wide_first = jnp.concatenate([columns[:half]] * (half // HD), axis=1)
+    halo_ok = (wide_first == 0.0) & (iota((half, half), 1).astype(F32) >= half - prev_count)
+    maskb[0, :, 0:half] = jnp.where(halo_ok, 0.0, NEG)
 
     ones_tok = jnp.ones((tok, HD), BF16)
     ones_ext = jnp.ones((HD, HD), BF16)
 
-    def window(h, b):
-        lanes = pl.ds(pl.multiple_of(h * HD, HD), HD)
-        q = qd[b * half : (b + 1) * half, lanes]
-        keys = kx[b * half : b * half + tok, lanes]
-        ext = jnp.concatenate([ekh[:, lanes], ekl[:, lanes]], axis=1)
-        s = jnp.concatenate(
-            [dot_nt(q, keys), dot_nt(jnp.concatenate([q, q], axis=1), ext)], axis=1
-        ) + maskb[b]
-        m = jnp.max(s, axis=1, keepdims=True)
-        p = jnp.exp2((s - m) * EXP_SCALE).astype(BF16)
-        v = jnp.concatenate([vx[b * half : b * half + tok, lanes], ones_tok], axis=1)
-        ev = jnp.concatenate([evv[:, lanes], ones_ext], axis=1)
-        acc[h, b * half : (b + 1) * half, :] = dot(p[:, :tok], v) + dot(p[:, tok:], ev)
-        mrow[h, b * half : (b + 1) * half, :] = jnp.broadcast_to(m, (half, HD))
+    def window(hs, b):
+        lo = half
+        count = half * (b + 1)
+        rows = slice(b * half, (b + 1) * half)
+        lanes = [pl.ds(pl.multiple_of(h * HD, HD), HD) for h in hs]
+        scores = []
+        for ln in lanes:
+            q = qd[rows, ln]
+            ext = jnp.concatenate([ekh[:, ln], ekl[:, ln]], axis=1)
+            scores.append(
+                jnp.concatenate(
+                    [dot_nt(q, kx[lo : lo + count, ln]),
+                     dot_nt(jnp.concatenate([q, q], axis=1), ext)], axis=1,
+                ) + maskb[b, :, tok - count :]
+            )
+        tops = [jnp.max(s, axis=1, keepdims=True) for s in scores]
+        probs = [jnp.exp2((s - m) * EXP_SCALE).astype(BF16) for s, m in zip(scores, tops)]
+        for h, ln, p, m in zip(hs, lanes, probs, tops):
+            v = jnp.concatenate([vx[lo : lo + count, ln], ones_tok[:count]], axis=1)
+            ev = jnp.concatenate([evv[:, ln], ones_ext], axis=1)
+            acc[h, rows, :] = dot(p[:, :count], v) + dot(p[:, count:], ev)
+            mrow[h, rows, :] = jnp.broadcast_to(m, (half, HD))
 
     def windows(lo, hi, b):
-        def body(h, _):
-            window(h, b)
+        def body(n, _):
+            window((2 * n, 2 * n + 1), b)
             return 0
 
-        lax.fori_loop(lo, hi, body, 0)
+        lax.fori_loop(lo // 2, hi // 2, body, 0)
 
     share = heads // steps
 
@@ -409,13 +420,9 @@
             if i < steps:
                 ring_start(i + 1)
 
-        run_if(if_core0(i), go)
+        run_if(here(i), go)
         row_start(i)
-        run_if(if_core0(i), lambda: pass_on(0, i).start())
-
-    for i in range(1, steps + 1):
-        landed(i)
-        windows((i - 1) * share, i * share, 1)
+        run_if(here(i), lambda: pass_on(0, i).start())
 
     def rows_landed(i):
         for dx in range(1, nx):
@@ -423,9 +430,18 @@
                 row_recv(dx, i).wait_recv()
                 pass_on(dx, i).start()
 
-            run_if(if_core0(i, xpos >= dx), go)
-
-    for i in range(0, steps - 1):
+            run_if(here(i, xpos >= dx), go)
+
+    windows(0, heads // 2, 1)
+    for i in range(1, steps + 1):
+        landed(i)
+        if i == 1:
+            windows(heads // 2, heads, 1)
+        elif i == 2:
+            windows(0, heads // 2, 0)
+        elif i == 3:
+            windows(heads // 2, heads, 0)
+    for i in range(0, steps + 1):
         rows_landed(i)
 
     @pl.when(d > 0)
@@ -433,14 +449,10 @@
         halo_copy(0, kx).wait_recv()
         halo_copy(1, vx).wait_recv()
 
-    windows(0, heads // 2, 0)
-    for i in range(steps - 1, steps + 1):
-        rows_landed(i)
-    windows(heads // 2, heads, 0)
     for dx in range(nx):
         for i in range(0 if dx else 1, steps + 1):
             run_if(
-                if_core1_partner(i, (xpos >= dx) if dx else None),
+                there(i, (xpos >= dx) if dx else None),
                 lambda: passed(dx, i).wait_recv(),
             )
 
@@ -457,15 +469,28 @@
         vlanes = pl.ds(pl.multiple_of(width + h * HD, HD), HD)
         keys = jnp.concatenate([tab[:, :, lanes].reshape(nkeys, HD), kaux[...]], axis=1)
         values = jnp.concatenate([tab[:, :, vlanes].reshape(nkeys, HD), ones_key], axis=1)
-        for b in range(2):
-            rows = slice(b * half, (b + 1) * half)
-            q = jnp.concatenate([qd[rows, lanes], qaux[...]], axis=1)
-            s = dot_nt(q, keys)
-            old = mrow[h, rows, :]
-            m = jnp.maximum(old, jnp.max(s, axis=1, keepdims=True))
-            fade = jnp.exp2((old - m) * EXP_SCALE)
-            p = jnp.exp2((s - jnp.concatenate([m] * (nkeys // HD), axis=1)) * EXP_SCALE)
-            o = dot(p.astype(BF16), values)
+        halo_values = jnp.concatenate([vx[0:half, lanes], ones_tok[:half]], axis=1)
+        blocks = [slice(b * half, (b + 1) * half) for b in range(2)]
+        scores = [
+            dot_nt(jnp.concatenate([qd[rows, lanes], qaux[...]], axis=1), keys)
+            for rows in blocks
+        ]
+        near = dot_nt(qd[0:half, lanes], kx[0:half, lanes]) + maskb[0, :, 0:half]
+        tops = [jnp.max(s, axis=1, keepdims=True) for s in scores]
+        tops[0] = jnp.maximum(tops[0], jnp.max(near, axis=1, keepdims=True))
+        olds = [mrow[h, rows, :] for rows in blocks]
+        tops = [jnp.maximum(old, m) for old, m in zip(olds, tops)]
+        fades = [jnp.exp2((old - m) * EXP_SCALE) for old, m in zip(olds, tops)]
+        probs = [
+            jnp.exp2((s - jnp.concatenate([m] * (nkeys // HD), axis=1)) * EXP_SCALE).astype(BF16)
+            for s, m in zip(scores, tops)
+        ]
+        near = jnp.exp2(
+            (near - jnp.concatenate([tops[0]] * (half // HD), axis=1)) * EXP_SCALE
+        ).astype(BF16)
+        sums = [dot(p, values) for p in probs]
+        sums[0] = sums[0] + dot(near, halo_values)
+        for rows, fade, o in zip(blocks, fades, sums):
             prior = acc[h, rows, :]
             top = prior[:, :HD] * fade + o[:, :HD]
             bottom = prior[:, HD:] * fade + o[:, HD:]
@@ -495,7 +520,7 @@
     norm = jnp.broadcast_to(norm, (HD, tok)).T
     for h in range(heads):
         out_ref[:, h * HD : (h + 1) * HD] = (
-            acc[h, :, 0:HD] * norm * gain_ref[:, h * HD : (h + 1) * HD]
+            acc[h, :, 0:HD] * norm
         ).astype(BF16)
 
     for copy in sends:
@@ -512,14 +537,14 @@
         halo_copy(1, vx).wait_send()
 
     for i in range(1, steps + 1):
-        run_if(if_core0(i), lambda: ring_send(i).wait_send())
+        run_if(here(i), lambda: ring_send(i).wait_send())
     for i in range(0, steps + 1):
         for dx in range(1, nx):
-            run_if(if_core0(i, xpos + dx < nx), lambda: row_send(dx, i).wait_send())
+            run_if(here(i, xpos + dx < nx), lambda: row_send(dx, i).wait_send())
         for dx in range(nx):
             if dx or i:
                 run_if(
-                    if_core0(i, (xpos >= dx) if dx else None),
+                    here(i, (xpos >= dx) if dx else None),
                     lambda: pass_on(dx, i).wait_send(),
                 )
     for n in range(ny - 1):
@@ -539,10 +564,10 @@
         hbm = pl.BlockSpec(memory_space=pl.ANY)
         vmem = pl.BlockSpec(memory_space=pltpu.VMEM)
         smem = pl.BlockSpec(memory_space=pltpu.SMEM)
-        return pl.pallas_call(
+        out = pl.pallas_call(
             functools.partial(kernel, (nx, nz, ny)),
             out_shape=jax.ShapeDtypeStruct((tok, width), BF16),
-            in_specs=[hbm, hbm, hbm, smem, vmem, vmem],
+            in_specs=[hbm, hbm, hbm, smem, vmem],
             out_specs=vmem,
             scratch_shapes=[
                 pltpu.VMEM((tok, width), BF16),
@@ -580,8 +605,9 @@
             name="attention",
         )(
             q_raw, k_raw, v_raw, block_scales,
-            segment_ids.reshape(1, tok), norm_gain.reshape(1, width),
+            segment_ids.reshape(1, tok),
         )
+        return (out.astype(F32) * norm_gain[None, :]).astype(BF16)
 
     in_specs = (
         P("seq", "head"),

time: 59.7 us -> 56.4 us (0.945)
  the two profiles are of different devices: /device:TPU:32 before, /device:TPU:4 now
where the time goes in v2:
time: 56.4 us; the launch traced here: 56.2 us
  Pallas kernels  53.8 us (95%)
  other arithmetic  2.44 us (4%)
    pallas_call x1, Pallas kernels, on_device(): pl.pallas_call(functools.partial(kernel, (nx, nz, ny)), out_shape=jax.Sha...  53.8 us
    convert_element_type x1, other arithmetic, on_device(): return (out.astype(F32) * norm_gain[None, :]).astype(BF16)  2.44 us

profile of v2, /device:TPU:4, one launch (start us, length us, event | category | flops | bytes accessed | tf_op | source)
XLA Modules:
  0.0 56.2 jit_solution(2467358121298076943)
XLA Ops:
  0.0 0.0 copy-start
  0.0 53.8 %attention.1 = bf16[512,1024]{1,0:T(8,128)(2,1)} custom-call(bf16[512,1024]{1,0:T(8,128)(2,1)} %q_hbm.1, bf16[512,1024]{1,0:T(8,128)(2,1)} %k_hbm.1, bf16[512,1024]{1,0:T(8,128)(2,1)} %v_hbm.1, f32[3,4,8]{2,1,0:T(4,128)} %scales.1, s32[1,512]{1,0:T(1,128)} %bitcast.1), custom_call_target="tpu_custom_call" | custom-call | tf_op jit(solution)/shard_map/attention/pallas_call | solution.py:567
  53.8 0.0 copy-done
  53.8 2.4 %multiply_convert_fusion = bf16[512,1024]{1,0:T(8,128)(2,1)} fusion(bf16[512,1024]{1,0:T(8,128)(2,1)} %attention.1, f32[1024]{0:T(1024)S(1)} %copy-done), kind=kLoop, calls=%fused_computation | loop fusion | flops 1572864 | bytes 2101248 | tf_op jit(solution)/shard_map/convert_element_type | solution.py:610
Async XLA Ops:
  0.0 53.8 %copy-start = (f32[1024]{0:T(1024)S(1)}, f32[1024]{0:T(1024)}, u32[]{:S(2)}) copy-start(f32[1024]{0:T(1024)} %param.11) | copy-start | bytes 12292

commit v3 on v2

--- a/solution.py
+++ b/solution.py
@@ -79,6 +79,12 @@
     xpeers = [at(lax.rem(xpos + n, nx), zpos, core) for n in range(1, nx)]
     zpeers = [at(xpos, znext, core), at(xpos, zprev, core)]
     ypeers = [lax.rem(y + n, ny) for n in range(1, ny)]
+    for r in range(1, nx):
+        @pl.when(xpos < r)
+        def _():
+            for o in range(pairs):
+                tab[o * nx + r] = jnp.zeros((16, tab.shape[2]), BF16)
+
     barrier = pltpu.get_barrier_semaphore()
     greeted = peers + nextg + prevg + xpeers + zpeers
     for peer in greeted:
@@ -183,11 +189,6 @@
     def _():
         pbuf[0, 1] = jnp.zeros((8, width), F32)
 
-    for r in range(1, nx):
-        @pl.when(xpos < r)
-        def _():
-            tab[r * pairs : (r + 1) * pairs] = jnp.zeros((pairs, 16, tab.shape[2]), BF16)
-
     columns = jnp.broadcast_to(local.astype(F32), (HD, tok)).T
     own_ids = local.astype(F32)
     for b in range(2):
@@ -252,43 +253,63 @@
     aux = jnp.where(l16 == 0, hi, jnp.where(l16 == 1, mid, jnp.where(l16 == 2, low, 0.0)))
     own_keys = lkf[...].astype(BF16)
     own_values = lvf[...].astype(BF16)
-    tab[group, :, 0:width] = own_keys
-    tab[group, :, width : 2 * width] = own_values
-    tab[group, :, 2 * width :] = aux.astype(BF16)
-
-    def chunk_copy(row_x, p, send_sem, recv_sem, target):
-        g = row_x * pairs + p
+    tab[xpos, :, 0:width] = own_keys
+    tab[xpos, :, width : 2 * width] = own_values
+    tab[xpos, :, 2 * width :] = aux.astype(BF16)
+
+    steps = pairs // 2
+
+    def place(row_x, i, c):
+        if i == 0 or i == steps:
+            return max(2 * i - 1, 0) * nx + row_x
+        return (2 * i - 1 + c) * nx + row_x
+
+    def chunk_copy(source, dest, send_sem, recv_sem, target):
         return pltpu.make_async_remote_copy(
-            src_ref=tab.at[g], dst_ref=tab.at[g], send_sem=send_sem, recv_sem=recv_sem,
-            device_id={"seq": target}, device_id_type=MESH,
+            src_ref=tab.at[source], dst_ref=tab.at[dest], send_sem=send_sem,
+            recv_sem=recv_sem, device_id={"seq": target}, device_id_type=MESH,
         )
 
-    def ring_pair(i, c_sgn):
-        return lax.rem(pair - c_sgn * i + 2 * pairs, pairs)
-
-    steps = pairs // 2
-
     def ring_send(i):
-        return chunk_copy(xpos, ring_pair(i - 1, sgn), zs.at[i - 1], zr.at[i - 1],
-                          at(xpos, znext, core))
-
-    def ring_recv(i):
-        return chunk_copy(xpos, ring_pair(i, sgn), zs.at[i - 1], zr.at[i - 1],
-                          at(xpos, znext, core))
-
-    def row_send(dx, i):
-        return chunk_copy(xpos, ring_pair(i, sgn), xs.at[dx - 1, i], xr.at[dx - 1, i],
-                          at(lax.rem(xpos + dx, nx), zpos, core))
-
-    def row_recv(dx, i):
-        return chunk_copy(xpos - dx, ring_pair(i, sgn), xs.at[dx - 1, i], xr.at[dx - 1, i],
-                          at(lax.rem(xpos + dx, nx), zpos, core))
+        return chunk_copy(place(xpos, i - 1, core), place(xpos, i, core), zs.at[i - 1],
+                          zr.at[i - 1], at(xpos, znext, core))
+
+    ring_recv = ring_send
+
+    own_edges = ((0, 0, 1, None), (1, 1, 0, 1), (1, 1, 2, None), (0, 0, 3, None), (2, 2, 3, None))
+    relay_edges = ((1, 0, 2, 0), (2, 1, 3, 0), (3, 0, 2, 1), (0, 1, 3, 1))
+    far_edges = ((0, 0, 2, None), (1, 1, 3, None))
+    direct_from = steps - 1
+
+    def owned(i):
+        if i < direct_from:
+            return own_edges
+        return tuple(e for e in own_edges if e != (1, 1, 0, 1)) + far_edges
+
+    def relayed(i):
+        return relay_edges if i < direct_from else ()
+
+    def edge_copy(edge, i):
+        _, r, to, _ = edge
+        n = (to - r) % nx - 1
+        n_slot = place(r, i, core)
+        return chunk_copy(n_slot, n_slot, xs.at[n, i], xr.at[n, i], at(to, zpos, core))
+
+    def edge_if(edge, i, end, fn):
+        cond = xpos == edge[end]
+        if edge[3] is not None:
+            if (i == 0 and edge[3] == 1) or (i == steps and edge[3] == 0):
+                return
+            cond = cond & (core == edge[3])
+        run_if(here(i, cond), fn)
 
     def pass_on(dx, i):
-        return chunk_copy(xpos - dx, ring_pair(i, sgn), ds.at[dx, i], dr.at[dx, i], partner)
+        n_slot = place(xpos - dx, i, core)
+        return chunk_copy(n_slot, n_slot, ds.at[dx, i], dr.at[dx, i], partner)
 
     def passed(dx, i):
-        return chunk_copy(xpos - dx, ring_pair(i, -sgn), ds.at[dx, i], dr.at[dx, i], partner)
+        n_slot = place(xpos - dx, i, 1 - core)
+        return chunk_copy(n_slot, n_slot, ds.at[dx, i], dr.at[dx, i], partner)
 
     def here(i, extra=None):
         conds = []
@@ -316,8 +337,8 @@
         run_if(here(i), lambda: ring_send(i).start())
 
     def row_start(i):
-        for dx in range(1, nx):
-            run_if(here(i, xpos + dx < nx), lambda: row_send(dx, i).start())
+        for edge in owned(i):
+            edge_if(edge, i, 0, lambda: edge_copy(edge, i).start())
 
     ring_start(1)
     row_start(0)
@@ -424,13 +445,17 @@
         row_start(i)
         run_if(here(i), lambda: pass_on(0, i).start())
 
-    def rows_landed(i):
-        for dx in range(1, nx):
+    def rows_landed(i, edges):
+        for edge in edges:
             def go():
-                row_recv(dx, i).wait_recv()
-                pass_on(dx, i).start()
-
-            run_if(here(i, xpos >= dx), go)
+                edge_copy(edge, i).wait_recv()
+                if edge[2] > edge[1]:
+                    pass_on(edge[2] - edge[1], i).start()
+
+            edge_if(edge, i, 2, go)
+            for relay in relayed(i):
+                if edge[0] == edge[1] and relay[:2] == (edge[2], edge[1]):
+                    edge_if(relay, i, 0, lambda: edge_copy(relay, i).start())
 
     windows(0, heads // 2, 1)
     for i in range(1, steps + 1):
@@ -441,65 +466,106 @@
             windows(0, heads // 2, 0)
         elif i == 3:
             windows(heads // 2, heads, 0)
-    for i in range(0, steps + 1):
-        rows_landed(i)
-
-    @pl.when(d > 0)
-    def _():
-        halo_copy(0, kx).wait_recv()
-        halo_copy(1, vx).wait_recv()
-
-    for dx in range(nx):
-        for i in range(0 if dx else 1, steps + 1):
-            run_if(
-                there(i, (xpos >= dx) if dx else None),
-                lambda: passed(dx, i).wait_recv(),
-            )
-
-    nkeys = ngroups * 16
-    flat_aux = tab[:, :, 2 * width :].reshape(nkeys, HD)
-    key_group = lax.div(iota((nkeys, HD), 0), 16)
+        rows_landed(i - 1, owned(i - 1))
+    for i in range(0, direct_from):
+        rows_landed(i, relayed(i))
+
+    def passed_wait(i, only=None):
+        for dx in range(nx):
+            if i == 0 and dx == 0:
+                continue
+            cond = (xpos >= dx) if dx else None
+            if only is not None:
+                cond = (core == 1 - only) if cond is None else cond & (core == 1 - only)
+            run_if(there(i, cond), lambda: passed(dx, i).wait_recv())
+
+    nkeys = ngroups * 8
+    key_slot = lax.div(iota((2 * nkeys, HD), 0), 16)
+    order = lax.div(key_slot, nx)
+    hop = lax.div(order + 1, 2)
+    key_pair = lax.rem(
+        jnp.where(lax.rem(order, 2) == 1, pair - hop, pair + hop) + pairs, pairs
+    )
+    visible_key = lax.rem(key_slot, nx) * pairs + key_pair < group
     off = jnp.where(iota((nkeys, HD), 1) == 0, NEG, 0.0)
-    kaux[...] = jnp.where(key_group < group, flat_aux.astype(F32), off).astype(BF16)
     squares[...] = jnp.zeros(squares.shape, F32)
     ones_key = jnp.ones((nkeys, HD), BF16)
-
-    def landmarks(h, _):
+    blocks = [slice(b * half, (b + 1) * half) for b in range(2)]
+
+    def mask_part(n):
+        flat_aux = tab[n * nkeys // 16 : (n + 1) * nkeys // 16, :, 2 * width :].reshape(nkeys, HD)
+        ok = visible_key[n * nkeys : (n + 1) * nkeys]
+        kaux[n * nkeys : (n + 1) * nkeys, :] = jnp.where(
+            ok, flat_aux.astype(F32), off
+        ).astype(BF16)
+
+    def landmarks(h, part):
         lanes = pl.ds(pl.multiple_of(h * HD, HD), HD)
         vlanes = pl.ds(pl.multiple_of(width + h * HD, HD), HD)
-        keys = jnp.concatenate([tab[:, :, lanes].reshape(nkeys, HD), kaux[...]], axis=1)
-        values = jnp.concatenate([tab[:, :, vlanes].reshape(nkeys, HD), ones_key], axis=1)
-        halo_values = jnp.concatenate([vx[0:half, lanes], ones_tok[:half]], axis=1)
-        blocks = [slice(b * half, (b + 1) * half) for b in range(2)]
+        slots = slice(part * nkeys // 16, (part + 1) * nkeys // 16)
+        aux_rows = kaux[part * nkeys : (part + 1) * nkeys, :]
+        keys = jnp.concatenate([tab[slots, :, lanes].reshape(nkeys, HD), aux_rows], axis=1)
+        values = jnp.concatenate([tab[slots, :, vlanes].reshape(nkeys, HD), ones_key], axis=1)
         scores = [
             dot_nt(jnp.concatenate([qd[rows, lanes], qaux[...]], axis=1), keys)
             for rows in blocks
         ]
-        near = dot_nt(qd[0:half, lanes], kx[0:half, lanes]) + maskb[0, :, 0:half]
-        tops = [jnp.max(s, axis=1, keepdims=True) for s in scores]
-        tops[0] = jnp.maximum(tops[0], jnp.max(near, axis=1, keepdims=True))
+        values = [values, values]
+        if part == 1:
+            near = dot_nt(qd[0:half, lanes], kx[0:half, lanes]) + maskb[0, :, 0:half]
+            scores[0] = jnp.concatenate([scores[0], near], axis=1)
+            near_values = jnp.concatenate([vx[0:half, lanes], ones_tok[:half]], axis=1)
+            values[0] = jnp.concatenate([values[0], near_values], axis=0)
         olds = [mrow[h, rows, :] for rows in blocks]
-        tops = [jnp.maximum(old, m) for old, m in zip(olds, tops)]
+        tops = [
+            jnp.maximum(old, jnp.max(s, axis=1, keepdims=True))
+            for old, s in zip(olds, scores)
+        ]
         fades = [jnp.exp2((old - m) * EXP_SCALE) for old, m in zip(olds, tops)]
         probs = [
-            jnp.exp2((s - jnp.concatenate([m] * (nkeys // HD), axis=1)) * EXP_SCALE).astype(BF16)
+            jnp.exp2(
+                (s - jnp.concatenate([m] * (s.shape[1] // HD), axis=1)) * EXP_SCALE
+            ).astype(BF16)
             for s, m in zip(scores, tops)
         ]
-        near = jnp.exp2(
-            (near - jnp.concatenate([tops[0]] * (half // HD), axis=1)) * EXP_SCALE
-        ).astype(BF16)
-        sums = [dot(p, values) for p in probs]
-        sums[0] = sums[0] + dot(near, halo_values)
-        for rows, fade, o in zip(blocks, fades, sums):
+        sums = [dot(p, v) for p, v in zip(probs, values)]
+        for rows, fade, m, o in zip(blocks, fades, tops, sums):
             prior = acc[h, rows, :]
             top = prior[:, :HD] * fade + o[:, :HD]
             bottom = prior[:, HD:] * fade + o[:, HD:]
-            a = top / bottom
-            acc[h, rows, 0:HD] = a
-            squares[rows, :] += a * a
-        return 0
-
-    lax.fori_loop(0, heads, landmarks, 0)
+            if part == 0:
+                mrow[h, rows, :] = m
+                acc[h, rows, 0:HD] = top
+                acc[h, rows, HD:] = bottom
+            else:
+                a = top / bottom
+                acc[h, rows, 0:HD] = a
+                squares[rows, :] += a * a
+
+    def landmark_pass(part):
+        def body(h, _):
+            landmarks(h, part)
+            return 0
+
+        mask_part(part)
+        lax.fori_loop(0, heads, body, 0)
+
+    early = max(steps // 2, 1)
+    for i in range(0, early):
+        passed_wait(i)
+    passed_wait(early, only=0)
+    landmark_pass(0)
+    rows_landed(steps, owned(steps))
+    passed_wait(early, only=1)
+    for i in range(early + 1, steps + 1):
+        passed_wait(i)
+
+    @pl.when(d > 0)
+    def _():
+        halo_copy(0, kx).wait_recv()
+        halo_copy(1, vx).wait_recv()
+
+    landmark_pass(1)
 
     ssbuf[0] = jnp.broadcast_to(jnp.sum(squares[...].T, axis=0, keepdims=True), (8, tok))
 
@@ -539,8 +605,8 @@
     for i in range(1, steps + 1):
         run_if(here(i), lambda: ring_send(i).wait_send())
     for i in range(0, steps + 1):
-        for dx in range(1, nx):
-            run_if(here(i, xpos + dx < nx), lambda: row_send(dx, i).wait_send())
+        for edge in owned(i) + relayed(i):
+            edge_if(edge, i, 0, lambda: edge_copy(edge, i).wait_send())
         for dx in range(nx):
             if dx or i:
                 run_if(
@@ -600,11 +666,12 @@
                 dma((max(ny - 1, 1),)), dma((max(ny - 1, 1),)),
             ],
             compiler_params=pltpu.CompilerParams(
-                collective_id=0, has_side_effects=True, vmem_limit_bytes=60000000
+                collective_id=0, has_side_effects=True, vmem_limit_bytes=28000000
             ),
             name="attention",
         )(
-            q_raw, k_raw, v_raw, block_scales,
+            *(pltpu.with_memory_space_constraint(a, pltpu.HBM) for a in (q_raw, k_raw, v_raw)),
+            block_scales,
             segment_ids.reshape(1, tok),
         )
         return (out.astype(F32) * norm_gain[None, :]).astype(BF16)

time: 56.4 us -> 58.3 us (1.034)
  Pallas kernels: 53.8 us -> 55.5 us
  local copies, waits for them, and re-layouts: 0.01 us -> 1.38 us
  other arithmetic: 2.44 us -> 1.22 us
    pallas_call x1, Pallas kernels: 53.8 us -> 55.5 us  [on_device(): pl.pallas_call(functools.partial(kernel, (nx, nz, ny)), out_shape=jax.Sha...]
    unnamed x2 -> x6, local copies, waits for them, and re-layouts: 0.01 us -> 1.38 us
    convert_element_type x1, other arithmetic: 2.44 us -> 1.22 us  [on_device(): return (out.astype(F32) * norm_gain[None, :]).astype(BF16)]
where the time goes in v3:
time: 58.3 us; the launch traced here: 58.1 us
  Pallas kernels  55.5 us (95%)
  local copies, waits for them, and re-layouts  1.38 us (2%)
  other arithmetic  1.22 us (2%)
    pallas_call x1, Pallas kernels, on_device(): pl.pallas_call(functools.partial(kernel, (nx, nz, ny)), out_shape=jax.Sha...  55.5 us
    unnamed x6, local copies, waits for them, and re-layouts  1.38 us
    convert_element_type x1, other arithmetic, on_device(): return (out.astype(F32) * norm_gain[None, :]).astype(BF16)  1.22 us

profile of v3, /device:TPU:4, one launch (start us, length us, event | category | flops | bytes accessed | tf_op | source)
XLA Modules:
  0.0 58.1 jit_solution(10122052144084544424)
XLA Ops:
  0.0 0.0 copy-start
  0.0 0.7 %copy-done = f32[3,4,8]{2,1,0:T(4,128)S(1)} copy-done((f32[3,4,8]{2,1,0:T(4,128)S(1)}, f32[3,4,8]{2,1,0:T(4,128)}, u32[]{:S(2)}) %copy-start) | copy-done | bytes 408
  0.7 0.0 copy-start.1
  0.7 0.7 %copy-done.1 = s32[512]{0:T(512)S(1)} copy-done((s32[512]{0:T(512)S(1)}, s32[512]{0:T(512)}, u32[]{:S(2)}) %copy-start.1) | copy-done | bytes 2072
  1.4 0.0 copy-start.2
  1.4 55.5 %attention.1 = bf16[512,1024]{1,0:T(8,128)(2,1)S(1)} custom-call(bf16[512,1024]{1,0:T(8,128)(2,1)} %q_hbm.1, bf16[512,1024]{1,0:T(8,128)(2,1)} %k_hbm.1, bf16[512,1024]{1,0:T(8,128)(2,1)} %v_hbm.1, f32[3,4,8]{2,1,0:T(4,128)S(1)} %copy-done, s32[1,512]{1,0:T(1,128)S(1)} %bitcast.1), custom_call_target="tpu_custom_call" | custom-call | tf_op jit(solution)/shard_map/attention/pallas_call | solution.py:633
  56.9 0.0 copy-done.2
  56.9 1.2 %multiply_convert_fusion = bf16[512,1024]{1,0:T(8,128)(2,1)} fusion(bf16[512,1024]{1,0:T(8,128)(2,1)S(1)} %attention.1, f32[1024]{0:T(1024)S(1)} %copy-done.2), kind=kLoop, calls=%fused_computation | loop fusion | flops 1572864 | bytes 2101248 | tf_op jit(solution)/shard_map/convert_element_type | solution.py:677
Async XLA Ops:
  0.0 0.7 %copy-start = (f32[3,4,8]{2,1,0:T(4,128)S(1)}, f32[3,4,8]{2,1,0:T(4,128)}, u32[]{:S(2)}) copy-start(f32[3,4,8]{2,1,0:T(4,128)} %scales.1) | copy-start | bytes 1156
  0.7 0.7 %copy-start.1 = (s32[512]{0:T(512)S(1)}, s32[512]{0:T(512)}, u32[]{:S(2)}) copy-start(s32[512]{0:T(512)} %param.10) | copy-start | bytes 6148
  1.4 55.5 %copy-start.2 = (f32[1024]{0:T(1024)S(1)}, f32[1024]{0:T(1024)}, u32[]{:S(2)}) copy-start(f32[1024]{0:T(1024)} %param.11) | copy-start | bytes 12292

commit v4 on v2

--- a/solution.py
+++ b/solution.py
@@ -79,6 +79,11 @@
     xpeers = [at(lax.rem(xpos + n, nx), zpos, core) for n in range(1, nx)]
     zpeers = [at(xpos, znext, core), at(xpos, zprev, core)]
     ypeers = [lax.rem(y + n, ny) for n in range(1, ny)]
+    for r in range(1, nx):
+        @pl.when(xpos < r)
+        def _():
+            tab[r * pairs : (r + 1) * pairs] = jnp.zeros((pairs, 16, tab.shape[2]), BF16)
+
     barrier = pltpu.get_barrier_semaphore()
     greeted = peers + nextg + prevg + xpeers + zpeers
     for peer in greeted:
@@ -183,11 +188,6 @@
     def _():
         pbuf[0, 1] = jnp.zeros((8, width), F32)
 
-    for r in range(1, nx):
-        @pl.when(xpos < r)
-        def _():
-            tab[r * pairs : (r + 1) * pairs] = jnp.zeros((pairs, 16, tab.shape[2]), BF16)
-
     columns = jnp.broadcast_to(local.astype(F32), (HD, tok)).T
     own_ids = local.astype(F32)
     for b in range(2):
@@ -276,13 +276,31 @@
         return chunk_copy(xpos, ring_pair(i, sgn), zs.at[i - 1], zr.at[i - 1],
                           at(xpos, znext, core))
 
-    def row_send(dx, i):
-        return chunk_copy(xpos, ring_pair(i, sgn), xs.at[dx - 1, i], xr.at[dx - 1, i],
-                          at(lax.rem(xpos + dx, nx), zpos, core))
-
-    def row_recv(dx, i):
-        return chunk_copy(xpos - dx, ring_pair(i, sgn), xs.at[dx - 1, i], xr.at[dx - 1, i],
-                          at(lax.rem(xpos + dx, nx), zpos, core))
+    own_edges = ((0, 0, 1, None), (1, 1, 0, 1), (1, 1, 2, None), (0, 0, 3, None), (2, 2, 3, None))
+    relay_edges = ((1, 0, 2, 0), (2, 1, 3, 0), (3, 0, 2, 1), (0, 1, 3, 1))
+    far_edges = ((0, 0, 2, None), (1, 1, 3, None))
+    direct_from = steps - 1
+
+    def owned(i):
+        if i < direct_from:
+            return own_edges
+        return tuple(e for e in own_edges if e != (1, 1, 0, 1)) + far_edges
+
+    def relayed(i):
+        return relay_edges if i < direct_from else ()
+
+    def edge_copy(edge, i):
+        _, r, to, _ = edge
+        n = (to - r) % nx - 1
+        return chunk_copy(r, ring_pair(i, sgn), xs.at[n, i], xr.at[n, i], at(to, zpos, core))
+
+    def edge_if(edge, i, end, fn):
+        cond = xpos == edge[end]
+        if edge[3] is not None:
+            if (i == 0 and edge[3] == 1) or (i == steps and edge[3] == 0):
+                return
+            cond = cond & (core == edge[3])
+        run_if(here(i, cond), fn)
 
     def pass_on(dx, i):
         return chunk_copy(xpos - dx, ring_pair(i, sgn), ds.at[dx, i], dr.at[dx, i], partner)
@@ -316,8 +334,8 @@
         run_if(here(i), lambda: ring_send(i).start())
 
     def row_start(i):
-        for dx in range(1, nx):
-            run_if(here(i, xpos + dx < nx), lambda: row_send(dx, i).start())
+        for edge in owned(i):
+            edge_if(edge, i, 0, lambda: edge_copy(edge, i).start())
 
     ring_start(1)
     row_start(0)
@@ -424,13 +442,17 @@
         row_start(i)
         run_if(here(i), lambda: pass_on(0, i).start())
 
-    def rows_landed(i):
-        for dx in range(1, nx):
+    def rows_landed(i, edges):
+        for edge in edges:
             def go():
-                row_recv(dx, i).wait_recv()
-                pass_on(dx, i).start()
-
-            run_if(here(i, xpos >= dx), go)
+                edge_copy(edge, i).wait_recv()
+                if edge[2] > edge[1]:
+                    pass_on(edge[2] - edge[1], i).start()
+
+            edge_if(edge, i, 2, go)
+            for relay in relayed(i):
+                if edge[0] == edge[1] and relay[:2] == (edge[2], edge[1]):
+                    edge_if(relay, i, 0, lambda: edge_copy(relay, i).start())
 
     windows(0, heads // 2, 1)
     for i in range(1, steps + 1):
@@ -441,8 +463,10 @@
             windows(0, heads // 2, 0)
         elif i == 3:
             windows(heads // 2, heads, 0)
-    for i in range(0, steps + 1):
-        rows_landed(i)
+        rows_landed(i - 1, owned(i - 1))
+    for i in range(0, direct_from):
+        rows_landed(i, relayed(i))
+    rows_landed(steps, owned(steps))
 
     @pl.when(d > 0)
     def _():
@@ -499,7 +523,7 @@
             squares[rows, :] += a * a
         return 0
 
-    lax.fori_loop(0, heads, landmarks, 0)
+    lax.fori_loop(0, heads, landmarks, 0, unroll=2)
 
     ssbuf[0] = jnp.broadcast_to(jnp.sum(squares[...].T, axis=0, keepdims=True), (8, tok))
 
@@ -539,8 +563,8 @@
     for i in range(1, steps + 1):
         run_if(here(i), lambda: ring_send(i).wait_send())
     for i in range(0, steps + 1):
-        for dx in range(1, nx):
-            run_if(here(i, xpos + dx < nx), lambda: row_send(dx, i).wait_send())
+        for edge in owned(i) + relayed(i):
+            edge_if(edge, i, 0, lambda: edge_copy(edge, i).wait_send())
         for dx in range(nx):
             if dx or i:
                 run_if(
@@ -600,11 +624,12 @@
                 dma((max(ny - 1, 1),)), dma((max(ny - 1, 1),)),
             ],
             compiler_params=pltpu.CompilerParams(
-                collective_id=0, has_side_effects=True, vmem_limit_bytes=60000000
+                collective_id=0, has_side_effects=True, vmem_limit_bytes=28000000
             ),
             name="attention",
         )(
-            q_raw, k_raw, v_raw, block_scales,
+            *(pltpu.with_memory_space_constraint(a, pltpu.HBM) for a in (q_raw, k_raw, v_raw)),
+            block_scales,
             segment_ids.reshape(1, tok),
         )
         return (out.astype(F32) * norm_gain[None, :]).astype(BF16)

time: 56.4 us -> 52.7 us (0.934)
  Pallas kernels: 53.8 us -> 49.4 us
  local copies, waits for them, and re-layouts: 0.01 us -> 1.38 us
  other arithmetic: 2.44 us -> 1.22 us
    pallas_call x1, Pallas kernels: 53.8 us -> 49.4 us  [on_device(): pl.pallas_call(functools.partial(kernel, (nx, nz, ny)), out_shape=jax.Sha...]
    unnamed x2 -> x6, local copies, waits for them, and re-layouts: 0.01 us -> 1.38 us
    convert_element_type x1, other arithmetic: 2.44 us -> 1.22 us  [on_device(): return (out.astype(F32) * norm_gain[None, :]).astype(BF16)]
where the time goes in v4:
time: 52.7 us; the launch traced here: 52 us
  Pallas kernels  49.4 us (94%)
  local copies, waits for them, and re-layouts  1.38 us (3%)
  other arithmetic  1.22 us (2%)
    pallas_call x1, Pallas kernels, on_device(): pl.pallas_call(functools.partial(kernel, (nx, nz, ny)), out_shape=jax.Sha...  49.4 us
    unnamed x6, local copies, waits for them, and re-layouts  1.38 us
    convert_element_type x1, other arithmetic, on_device(): return (out.astype(F32) * norm_gain[None, :]).astype(BF16)  1.22 us

profile of v4, /device:TPU:4, one launch (start us, length us, event | category | flops | bytes accessed | tf_op | source)
XLA Modules:
  0.0 52.0 jit_solution(11795319620582584428)
XLA Ops:
  0.0 0.0 copy-start
  0.0 0.7 %copy-done = f32[3,4,8]{2,1,0:T(4,128)S(1)} copy-done((f32[3,4,8]{2,1,0:T(4,128)S(1)}, f32[3,4,8]{2,1,0:T(4,128)}, u32[]{:S(2)}) %copy-start) | copy-done | bytes 408
  0.7 0.0 copy-start.1
  0.7 0.7 %copy-done.1 = s32[512]{0:T(512)S(1)} copy-done((s32[512]{0:T(512)S(1)}, s32[512]{0:T(512)}, u32[]{:S(2)}) %copy-start.1) | copy-done | bytes 2072
  1.4 0.0 copy-start.2
  1.4 49.4 %attention.1 = bf16[512,1024]{1,0:T(8,128)(2,1)S(1)} custom-call(bf16[512,1024]{1,0:T(8,128)(2,1)} %q_hbm.1, bf16[512,1024]{1,0:T(8,128)(2,1)} %k_hbm.1, bf16[512,1024]{1,0:T(8,128)(2,1)} %v_hbm.1, f32[3,4,8]{2,1,0:T(4,128)S(1)} %copy-done, s32[1,512]{1,0:T(1,128)S(1)} %bitcast.1), custom_call_target="tpu_custom_call" | custom-call | tf_op jit(solution)/shard_map/attention/pallas_call | solution.py:591
  50.8 0.0 copy-done.2
  50.8 1.2 %multiply_convert_fusion = bf16[512,1024]{1,0:T(8,128)(2,1)} fusion(bf16[512,1024]{1,0:T(8,128)(2,1)S(1)} %attention.1, f32[1024]{0:T(1024)S(1)} %copy-done.2), kind=kLoop, calls=%fused_computation | loop fusion | flops 1572864 | bytes 2101248 | tf_op jit(solution)/shard_map/convert_element_type | solution.py:635
Async XLA Ops:
  0.0 0.7 %copy-start = (f32[3,4,8]{2,1,0:T(4,128)S(1)}, f32[3,4,8]{2,1,0:T(4,128)}, u32[]{:S(2)}) copy-start(f32[3,4,8]{2,1,0:T(4,128)} %scales.1) | copy-start | bytes 1156
  0.7 0.7 %copy-start.1 = (s32[512]{0:T(512)S(1)}, s32[512]{0:T(512)}, u32[]{:S(2)}) copy-start(s32[512]{0:T(512)} %param.10) | copy-start | bytes 6148
  1.4 49.4 %copy-start.2 = (f32[1024]{0:T(1024)S(1)}, f32[1024]{0:T(1024)}, u32[]{:S(2)}) copy-start(f32[1024]{0:T(1024)} %param.11) | copy-start | bytes 12292
